TPU v7x, 16 devices: a 4x2x1 block of a 4x4x8 slice. The times are simulated.
16 devices in a mesh: dp: 4 (over y, z, core), tp: 4 (over x).
Axes of the slice: x: 4, y: 2, z: 1, core: 2. Of those that a mesh axis runs over, the one named last changes fastest.
The devices are a block of a 4x4x8 slice.
Arguments:
- x: bfloat16 [512, 4096], P('dp'), parts along dimension 0
- w_gate: bfloat16 [4096, 10240], P(None, 'tp')
- w_up: bfloat16 [4096, 10240], P(None, 'tp')
- w_down: bfloat16 [10240, 4096], P('tp')
Outputs:
- output: bfloat16 [512, 4096], P('dp'), parts along dimension 0
There are 4 independent parts. A program takes and returns all parts, laid end to end along the dimension named above; an argument that names none is the same for every part.
All inputs are finite; a program needn't handle non-finite values.
Results may differ from a plain program's by a relative error of at most 0.016.
Values are sent between devices in bfloat16 or wider.
A program may use at most 768 MiB of HBM per device.

v0:
```python
import jax
import jax.numpy as jnp
from jax import lax
from jax.sharding import PartitionSpec as P


def solution(mesh):
    def step(x, w_gate, w_up, w_down):
        gate = jnp.dot(x, w_gate, preferred_element_type=jnp.float32)
        up = jnp.dot(x, w_up, preferred_element_type=jnp.float32)
        hidden = (jax.nn.gelu(gate) * up).astype(jnp.bfloat16)
        term = jnp.dot(hidden, w_down, preferred_element_type=jnp.float32).astype(jnp.bfloat16)
        return lax.psum(term, "tp")

    return jax.shard_map(
        step,
        mesh=mesh,
        in_specs=(P("dp", None), P(None, "tp"), P(None, "tp"), P("tp", None)),
        out_specs=P("dp", None),
        check_vma=False,
    )
```

profile of v0, /device:TPU:112, one launch (start us, length us, event | category | flops | bytes accessed | tf_op | source)
XLA Modules:
  0.0 84.0 jit_solution(2402744404484688431)
XLA Ops:
  6.5 0.0 copy-start
  6.6 0.0 all-reduce.2.cloned.1.call-start
  6.6 1.2 %copy-done = bf16[128,4096]{1,0:T(8,128)(2,1)S(1)} copy-done((bf16[128,4096]{1,0:T(8,128)(2,1)S(1)}, bf16[128,4096]{1,0:T(8,128)(2,1)}, u32[]{:S(2)}) %copy-start) | copy-done | bytes 1048600
  7.8 8.5 %fusion.8 = f32[128,2560]{1,0:T(8,128)S(1)} fusion(bf16[128,4096]{1,0:T(8,128)(2,1)S(1)} %copy-done, bf16[4096,2560]{1,0:T(8,128)(2,1)} %param.5), kind=kOutput, calls=%fused_computation.11 | convolution fusion | flops 2684354560 | bytes 23330816 | tf_op jit(solution)/shard_map/dot_general | solution.py:9
  16.3 17.6 %convolution_convert_fusion = bf16[128,4096]{1,0:T(8,128)(2,1)} fusion(bf16[2560,4096]{1,0:T(8,128)(2,1)} %param.7, bf16[128,4096]{1,0:T(8,128)(2,1)S(1)} %copy-done, bf16[4096,2560]{1,0:T(8,128)(2,1)} %param.6, f32[128,2560]{1,0:T(8,128)S(1)} %fusion.8), kind=kOutput, calls=%fused_computation | convolution fusion | flops 5372510208 | bytes 45350912 | tf_op jit(solution)/shard_map/dot_general | solution.py:12
  33.9 0.1 all-reduce.2.cloned.1.call-update
  34.0 0.0 copy-start.1
  34.0 40.8 %all-reduce.2.cloned.1.call-done = bf16[128,4096]{1,0:T(8,128)(2,1)} async-done(((bf16[128,4096]{1,0:T(8,128)(2,1)}), bf16[128,4096]{1,0:T(8,128)(2,1)}) %all-reduce.2.cloned.1.call-update) | async-done | bytes 1048592 | tf_op jit(solution)/shard_map/psum | solution.py:13
  74.8 2.3 %copy.6 = bf16[128,4096]{1,0:T(8,128)(2,1)} copy(bf16[128,4096]{1,0:T(8,128)(2,1)} %all-reduce.2.cloned.1.call-done) | data formatting | bytes 2097152
  77.1 0.0 copy-done.1
Async XLA Ops:
  6.5 1.2 %copy-start = (bf16[128,4096]{1,0:T(8,128)(2,1)S(1)}, bf16[128,4096]{1,0:T(8,128)(2,1)}, u32[]{:S(2)}) copy-start(bf16[128,4096]{1,0:T(8,128)(2,1)} %param.4) | copy-start | bytes 3145732
  6.6 68.3 %all-reduce.2.cloned.1.call-start = ((), (), s32[]{:S(2)}) async-start(), calls=%async_computation | async-start | bytes 2097152 | tf_op jit(solution)/shard_map/psum | solution.py:13
  34.0 43.1 %copy-start.1 = (bf16[128,4096]{1,0:T(8,128)(2,1)S(1)}, bf16[128,4096]{1,0:T(8,128)(2,1)}, u32[]{:S(2)}) copy-start(bf16[128,4096]{1,0:T(8,128)(2,1)} %param.4) | copy-start | bytes 3145732
Sparse Core Ops, SparseCore 0:
  34.1 40.6 all-reduce.1
where the time goes:
time: 84.1 us; the launch traced here: 84 us
  waiting for transfers between devices  40.9 us (49%)
  matrix products  26.2 us (31%)
  between operations  13.4 us (16%)
  local copies, waits for them, and re-layouts  3.52 us (4%)
    psum x1, waiting for transfers between devices, step(): return lax.psum(term, 'tp')  40.8 us
    dot_general x1, matrix products, step(): jnp.dot(hidden, w_down, preferred_element_type=jnp.float32)  17.6 us
    dot_general x1, matrix products, step(): gate = jnp.dot(x, w_gate, preferred_element_type=jnp.float32)  8.52 us
    unnamed x5, local copies, waits for them, and re-layouts  3.52 us
  transfers between devices with their start and end apart: 1, of which 1 were waited for; matrix products, arithmetic and copies ran while one was open for 0% of the time, Pallas kernels for 0%

commit v1 on v0

v1 whole, which is shorter than its diff:
```python
import functools

import jax
import jax.numpy as jnp
from jax import lax
from jax.experimental import pallas as pl
from jax.experimental.pallas import tpu as pltpu
from jax.sharding import PartitionSpec as P

MESH = pl.DeviceIdType.MESH
BF16 = jnp.bfloat16
F32 = jnp.float32
TK = 256
TN = 256
XP = 4
FAR, NEAR, CARRY = 0, 1, 2
RIGHT, LEFT = 0, 1


def kernel(
    n, x_hbm, wg_hbm, wu_hbm, wd_hbm, y_ref,
    xv, wgu, wd, gacc, hid, yacc, stage, recv, yb,
    x_sem, xs_send, xs_recv, w_sem, d_sem, h_send, h_recv,
    rs_send, rs_recv, ag_send, ag_recv, fw_send, fw_recv, own_send, own_recv,
):
    t = lax.axis_index("tp")
    g = lax.axis_index("dp")
    core = lax.rem(g, 2)
    base = g - core
    other = base + 1 - core
    right, left = lax.rem(t + 1, n), lax.rem(t + n - 1, n)
    far = lax.rem(t + 2, n)
    rows, depth = x_hbm.shape
    half = wg_hbm.shape[1] // 2
    steps = half // TK
    cols = wd_hbm.shape[1] // 2
    block = cols // n
    to = (right, left)

    def dev(tp, dp):
        return {"tp": tp, "dp": dp}

    def remote(src, dst, send, rcv, device):
        return pltpu.make_async_remote_copy(
            src_ref=src, dst_ref=dst, send_sem=send, recv_sem=rcv,
            device_id=device, device_id_type=MESH,
        )

    mine = pl.ds(pl.multiple_of(core * rows, rows), rows)
    his = pl.ds(pl.multiple_of((1 - core) * rows, rows), rows)
    x_load = pltpu.make_async_copy(x_hbm, xv.at[mine, :], x_sem)
    x_load.start()
    first = core * half
    w_loads = []
    for j in range(steps):
        at = pl.ds(pl.multiple_of(first + j * TK, TK), TK)
        w_loads.append((
            pltpu.make_async_copy(wg_hbm.at[:, at], wgu.at[j, :, :TK], w_sem.at[j, 0]),
            pltpu.make_async_copy(wu_hbm.at[:, at], wgu.at[j, :, TK:], w_sem.at[j, 1]),
        ))
    order = ((far, 0), (far, 1), (right, 1), (left, 0), (right, 0), (left, 1), (t, 0), (t, 1))
    d_loads = []
    for s, (owner, h) in enumerate(order):
        at = pl.ds(pl.multiple_of(core * cols + owner * block + h * TN, TN), TN)
        d_loads.append((
            pltpu.make_async_copy(
                wd_hbm.at[pl.ds(pl.multiple_of(core * half, half), half), at],
                wd.at[s, :half, :], d_sem.at[s, 0]),
            pltpu.make_async_copy(
                wd_hbm.at[pl.ds(pl.multiple_of((1 - core) * half, half), half), at],
                wd.at[s, half:, :], d_sem.at[s, 1]),
        ))
    for pair in w_loads + d_loads:
        for copy in pair:
            copy.start()

    barrier = pltpu.get_barrier_semaphore()
    partners = [dev(t, other)] + [dev(a, b) for a in to for b in (g, other)]
    for p in partners:
        pl.semaphore_signal(barrier, inc=1, device_id=p, device_id_type=MESH)
    pl.semaphore_wait(barrier, len(partners))

    x_load.wait()
    x_moves = []
    for k in range(XP):
        at = pl.ds(k * (depth // XP), depth // XP)
        x_moves.append(remote(xv.at[mine, at], xv.at[mine, at], xs_send.at[k], xs_recv.at[k], dev(t, other)))
        x_moves[-1].start()

    def gate_up(j, r):
        gacc[j % 2, r, :] = jnp.dot(xv[r, :], wgu[j], preferred_element_type=F32)

    h_moves = []

    def activate(j):
        a = gacc[j % 2]
        at = pl.ds(j * TK, TK)
        hid[:, at] = (jax.nn.gelu(a[:, :TK]) * a[:, TK:]).astype(BF16)
        h_moves.append(remote(
            hid.at[:, at], hid.at[:, pl.ds(half + j * TK, TK)], h_send.at[j], h_recv.at[j], dev(t, other)))
        h_moves[-1].start()

    for j in range(steps):
        for copy in w_loads[j]:
            copy.wait()
        if j == 0:
            gate_up(0, mine)
            for k in range(XP):
                at = pl.ds(k * (depth // XP), depth // XP)
                remote(xv.at[his, at], xv.at[his, at], xs_send.at[k], xs_recv.at[k], dev(t, other)).wait_recv()
            gate_up(0, his)
        else:
            gate_up(j, slice(None))
            activate(j - 1)
    activate(steps - 1)
    for move in h_moves:
        move.wait_recv()

    sends = []

    def hop(kind, d, p):
        i = (kind * 2 + d) * 2 + p
        return remote(stage.at[i], recv.at[i], rs_send.at[i], rs_recv.at[i], dev(to[d], g))

    def put(kind, d, p, v):
        i = (kind * 2 + d) * 2 + p
        stage[i] = v.astype(BF16)
        move = hop(kind, d, p)
        move.start()
        sends.append(move)

    def part(p):
        return slice(p * rows, (p + 1) * rows)

    for s, (kind, d) in enumerate(((FAR, RIGHT), (FAR, LEFT), (NEAR, RIGHT), (NEAR, LEFT))):
        for copy in d_loads[s]:
            copy.wait()
        v = jnp.dot(hid[...], wd[s], preferred_element_type=F32)
        if kind == FAR:
            for p in (0, 1):
                put(kind, d, p, v[part(p)])
        else:
            put(kind, d, 0, v[part(0)])
            i = (kind * 2 + d) * 2 + 1
            stage[i] = v[part(1)].astype(BF16)
    for s in range(4, 8):
        for copy in d_loads[s]:
            copy.wait()
        yacc[s - 4] = jnp.dot(hid[...], wd[s], preferred_element_type=F32)

    def got(kind, d, p):
        hop(kind, d, p).wait_recv()
        return recv[(kind * 2 + d) * 2 + p].astype(F32)

    for p in (0, 1):
        for d in (RIGHT, LEFT):
            put(CARRY, d, p, yacc[d, part(p), :] + got(FAR, d, p))
        if p == 0:
            for d in (RIGHT, LEFT):
                move = hop(NEAR, d, 1)
                move.start()
                sends.append(move)

    def place(k, owner, h, width):
        return pl.ds(pl.multiple_of(k * cols + owner * block + h * TN, TN), width)

    for p in (0, 1):
        yb[p, :, :TN] = (yacc[2, part(p), :] + got(CARRY, RIGHT, p) + got(NEAR, LEFT, p)).astype(BF16)
        for d, h in ((RIGHT, 0),):
            move = remote(yb.at[p, :, pl.ds(h * TN, TN)], y_ref.at[:, place(core, t, h, TN)],
                          ag_send.at[p, d, h], ag_recv.at[d, h, core], dev(to[d], base + p))
            move.start()
            sends.append(move)
        yb[p, :, TN:] = (yacc[3, part(p), :] + got(CARRY, LEFT, p) + got(NEAR, RIGHT, p)).astype(BF16)
        for d, h in ((LEFT, 1), (RIGHT, 1), (LEFT, 0)):
            move = remote(yb.at[p, :, pl.ds(h * TN, TN)], y_ref.at[:, place(core, t, h, TN)],
                          ag_send.at[p, d, h], ag_recv.at[d, h, core], dev(to[d], base + p))
            move.start()
            sends.append(move)

        @pl.when(core == p)
        def _():
            y_ref[:, place(core, t, 0, block)] = yb[p]

        @pl.when(core != p)
        def _():
            remote(yb.at[p], y_ref.at[:, place(core, t, 0, block)], own_send, own_recv, dev(t, other)).start()

    def landed(d, h, k):
        owner = (left, right)[d]
        at = place(k, owner, h, TN)
        return remote(y_ref.at[:, at], y_ref.at[:, at], ag_send.at[0, d, h], ag_recv.at[d, h, k], dev(to[d], g))

    for k in (0, 1):
        for d, h in ((RIGHT, 0), (LEFT, 1)):
            landed(d, h, k).wait_recv()
            at = place(k, (left, right)[d], h, TN)
            move = remote(y_ref.at[:, at], y_ref.at[:, at], fw_send.at[d, k], fw_recv.at[d, k], dev(to[d], g))
            move.start()
            sends.append(move)
    for k in (0, 1):
        for d, h in ((RIGHT, 1), (LEFT, 0)):
            landed(d, h, k).wait_recv()
    at = place(1 - core, t, 0, block)
    sib = remote(yb.at[0], y_ref.at[:, at], own_send, own_recv, dev(t, other))
    sib.wait_recv()
    for k in (0, 1):
        for d, h in ((RIGHT, 0), (LEFT, 1)):
            at = place(k, far, h, TN)
            remote(y_ref.at[:, at], y_ref.at[:, at], fw_send.at[d, k], fw_recv.at[d, k], dev(to[d], g)).wait_recv()
    sib.wait_send()
    for move in x_moves + h_moves + sends:
        move.wait_send()


def solution(mesh):
    n = mesh.shape["tp"]

    def step(x, w_gate, w_up, w_down):
        rows, depth = x.shape
        hidden, out = w_down.shape
        half, cols = hidden // 2, out // 2
        steps, pieces = half // TK, cols // TN
        DMA = pltpu.SemaphoreType.DMA
        any_spec = pl.BlockSpec(memory_space=pl.ANY)
        return pl.pallas_call(
            functools.partial(kernel, n),
            out_shape=jax.ShapeDtypeStruct((rows, out), BF16),
            in_specs=[any_spec] * 4,
            out_specs=pl.BlockSpec(memory_space=pltpu.VMEM),
            scratch_shapes=[
                pltpu.VMEM((2 * rows, depth), BF16),
                pltpu.VMEM((steps, depth, 2 * TK), BF16),
                pltpu.VMEM((pieces, hidden, TN), BF16),
                pltpu.VMEM((2, 2 * rows, 2 * TK), F32),
                pltpu.VMEM((2 * rows, hidden), BF16),
                pltpu.VMEM((4, 2 * rows, TN), F32),
                pltpu.VMEM((12, rows, TN), BF16),
                pltpu.VMEM((12, rows, TN), BF16),
                pltpu.VMEM((2, rows, 2 * TN), BF16),
                DMA, DMA((XP,)), DMA((XP,)), DMA((steps, 2)), DMA((pieces, 2)), DMA((steps,)), DMA((steps,)),
                DMA((12,)), DMA((12,)), DMA((2, 2, 2)), DMA((2, 2, 2)), DMA((2, 2)), DMA((2, 2)), DMA, DMA,
            ],
            compiler_params=pltpu.CompilerParams(
                collective_id=0, has_side_effects=True, vmem_limit_bytes=56 * 1024 * 1024
            ),
        )(x, w_gate, w_up, w_down)

    return jax.shard_map(
        step,
        mesh=mesh,
        in_specs=(P("dp", None), P(None, "tp"), P(None, "tp"), P("tp", None)),
        out_specs=P("dp", None),
        check_vma=False,
    )
```

time: 84.1 us -> 48.6 us (0.58)
  the two profiles are of different devices: /device:TPU:112 before, /device:TPU:113 now
where the time goes in v1:
time: 48.6 us; the launch traced here: 48.5 us
  Pallas kernels  46.2 us (95%)
  local copies, waits for them, and re-layouts  2.29 us (5%)
    pallas_call x1, Pallas kernels, step(): pl.pallas_call(functools.partial(kernel, n), out_shape=jax.ShapeDtypeStru...  46.2 us
    unnamed x1, local copies, waits for them, and re-layouts  2.29 us

profile of v1, /device:TPU:113, one launch (start us, length us, event | category | flops | bytes accessed | tf_op | source)
XLA Modules:
  0.0 48.5 jit_solution(1262892628629010465)
XLA Ops:
  0.0 46.2 %shard_map.46 = bf16[128,4096]{1,0:T(8,128)(2,1)} custom-call(bf16[128,4096]{1,0:T(8,128)(2,1)} %x_hbm.1, bf16[4096,2560]{1,0:T(8,128)(2,1)} %wg_hbm.1, bf16[4096,2560]{1,0:T(8,128)(2,1)} %wu_hbm.1, bf16[2560,4096]{1,0:T(8,128)(2,1)} %wd_hbm.1), custom_call_target="tpu_custom_call" | custom-call | tf_op jit(solution)/shard_map/pallas_call | solution.py:226
  46.2 2.3 %copy.6 = bf16[128,4096]{1,0:T(8,128)(2,1)} copy(bf16[128,4096]{1,0:T(8,128)(2,1)} %shard_map.46) | data formatting | bytes 2097152

commit v2 on v1

v2 whole, which is shorter than its diff:
```python
import functools

import jax
import jax.numpy as jnp
from jax import lax
from jax.experimental import pallas as pl
from jax.experimental.pallas import tpu as pltpu
from jax.sharding import PartitionSpec as P

MESH = pl.DeviceIdType.MESH
BF16 = jnp.bfloat16
F32 = jnp.float32
TK = 256
TN = 256
XP = 4
FAR, NEAR, CARRY = 0, 1, 2
RIGHT, LEFT = 0, 1


def kernel(
    n, x_hbm, wg_hbm, wu_hbm, wd_hbm, y_ref,
    xv, wgu, wd, gacc, hid, yacc, carry, stage, recv, yb,
    x_sem, xs_send, xs_recv, w_sem, d_sem, h_send, h_recv,
    rs_send, rs_recv, ag_send, ag_recv, fw_send, fw_recv, own_send, own_recv,
):
    t = lax.axis_index("tp")
    g = lax.axis_index("dp")
    core = lax.rem(g, 2)
    base = g - core
    other = base + 1 - core
    right, left = lax.rem(t + 1, n), lax.rem(t + n - 1, n)
    far = lax.rem(t + 2, n)
    rows, depth = x_hbm.shape
    half = wg_hbm.shape[1] // 2
    steps = half // TK
    cols = wd_hbm.shape[1] // 2
    block = cols // n
    to = (right, left)

    def dev(tp, dp):
        return {"tp": tp, "dp": dp}

    def remote(src, dst, send, rcv, device):
        return pltpu.make_async_remote_copy(
            src_ref=src, dst_ref=dst, send_sem=send, recv_sem=rcv,
            device_id=device, device_id_type=MESH,
        )

    mine = pl.ds(pl.multiple_of(core * rows, rows), rows)
    his = pl.ds(pl.multiple_of((1 - core) * rows, rows), rows)
    pieces = [pl.ds(k * (depth // XP), depth // XP) for k in range(XP)]
    x_loads = [pltpu.make_async_copy(x_hbm.at[:, at], xv.at[mine, at], x_sem.at[k]) for k, at in enumerate(pieces)]
    for copy in x_loads:
        copy.start()
    first = core * half
    w_loads = []
    for j in range(steps):
        at = pl.ds(pl.multiple_of(first + j * TK, TK), TK)
        w_loads.append((
            pltpu.make_async_copy(wg_hbm.at[:, at], wgu.at[j, :, :TK], w_sem.at[j, 0]),
            pltpu.make_async_copy(wu_hbm.at[:, at], wgu.at[j, :, TK:], w_sem.at[j, 1]),
        ))
    order = (far, right, left, t)
    d_loads = []
    for s, owner in enumerate(order):
        at = pl.ds(pl.multiple_of(core * cols + owner * block, block), block)
        d_loads.append((
            pltpu.make_async_copy(
                wd_hbm.at[pl.ds(pl.multiple_of(core * half, half), half), at],
                wd.at[s, :half, :], d_sem.at[s, 0]),
            pltpu.make_async_copy(
                wd_hbm.at[pl.ds(pl.multiple_of((1 - core) * half, half), half), at],
                wd.at[s, half:, :], d_sem.at[s, 1]),
        ))

    def start(copies):
        for copy in copies:
            copy.start(priority=1)

    for pair in w_loads:
        start(pair)

    barrier = pltpu.get_barrier_semaphore()
    partners = [dev(t, other)] + [dev(a, b) for a in to for b in (g, other)]
    for p in partners:
        pl.semaphore_signal(barrier, inc=1, device_id=p, device_id_type=MESH)
    pl.semaphore_wait(barrier, len(partners))
    x_moves = []
    for k, at in enumerate(pieces):
        x_loads[k].wait()
        x_moves.append(remote(xv.at[mine, at], xv.at[mine, at], xs_send.at[k], xs_recv.at[k], dev(t, other)))
        x_moves[-1].start()

    def gate_up(j, r):
        gacc[j % 2, r, :] = jnp.dot(xv[r, :], wgu[j], preferred_element_type=F32)

    h_moves = []

    def activate(j):
        a = gacc[j % 2]
        at = pl.ds(j * TK, TK)
        hid[:, at] = (jax.nn.gelu(a[:, :TK]) * a[:, TK:]).astype(BF16)
        h_moves.append(remote(
            hid.at[:, at], hid.at[:, pl.ds(half + j * TK, TK)], h_send.at[j], h_recv.at[j], dev(t, other)))
        h_moves[-1].start()

    def wait(copies, name):
        with jax.named_scope(name):
            for copy in copies:
                copy.wait()

    wait(w_loads[0], "w0")
    gate_up(0, mine)
    wait(w_loads[1], "w1")
    for k, at in enumerate(pieces):
        with jax.named_scope("waitx"):
            remote(xv.at[his, at], xv.at[his, at], xs_send.at[k], xs_recv.at[k], dev(t, other)).wait_recv()
    gate_up(0, his)
    for j in range(1, steps):
        if j > 1:
            wait(w_loads[j], f"w{j}")
            start(d_loads[j - 2])
            if j == steps - 1:
                start(d_loads[3])
        gate_up(j, slice(None))
        activate(j - 1)
    activate(steps - 1)

    sends = []

    def hop(kind, d, p):
        i = (kind * 2 + d) * 2 + p
        return remote(stage.at[i], recv.at[i], rs_send.at[i], rs_recv.at[i], dev(to[d], g))

    def put(kind, d, p, v):
        i = (kind * 2 + d) * 2 + p
        stage[i] = v.astype(BF16)

    def send(kind, d, p):
        move = hop(kind, d, p)
        move.start()
        sends.append(move)

    def part(p):
        return slice(p * rows, (p + 1) * rows)

    most = 2 * half - TK
    wait(d_loads[0], "d0")
    for j in range(steps - 1):
        with jax.named_scope("h"):
            h_moves[j].wait_recv()
    yacc[...] = jnp.dot(hid[:, :most], wd[0, :most, :], preferred_element_type=F32)
    with jax.named_scope("hlast"):
        h_moves[steps - 1].wait_recv()
    v = yacc[...] + jnp.dot(hid[:, most:], wd[0, most:, :], preferred_element_type=F32)
    for p in (0, 1):
        for d in (RIGHT, LEFT):
            put(FAR, d, p, v[part(p), d * TN : (d + 1) * TN])
            send(FAR, d, p)
    for d in (RIGHT, LEFT):
        wait(d_loads[1 + d], f"d{1 + d}")
        v = jnp.dot(hid[...], wd[1 + d], preferred_element_type=F32)
        for p in (0, 1):
            put(NEAR, d, p, v[part(p), (1 - d) * TN : (2 - d) * TN])
        send(NEAR, d, 0)
        carry[d] = v[:, d * TN : (d + 1) * TN]
    wait(d_loads[3], "d3")
    yacc[...] = jnp.dot(hid[...], wd[3], preferred_element_type=F32)

    def got(kind, d, p):
        with jax.named_scope(f"got{kind}{d}{p}"):
            hop(kind, d, p).wait_recv()
        return recv[(kind * 2 + d) * 2 + p].astype(F32)

    for p in (0, 1):
        for d in (RIGHT, LEFT):
            put(CARRY, d, p, carry[d, part(p), :] + got(FAR, d, p))
            send(CARRY, d, p)
        if p == 0:
            for d in (RIGHT, LEFT):
                send(NEAR, d, 1)

    def place(k, owner, h, width):
        return pl.ds(pl.multiple_of(k * cols + owner * block + h * TN, TN), width)

    def share(p, d, h):
        move = remote(yb.at[p, :, pl.ds(h * TN, TN)], y_ref.at[:, place(core, t, h, TN)],
                      ag_send.at[p, d, h], ag_recv.at[d, h, core], dev(to[d], base + p))
        move.start()
        sends.append(move)

    for p in (0, 1):
        for d in (RIGHT, LEFT):
            at = slice(d * TN, (d + 1) * TN)
            yb[p, :, at] = (yacc[part(p), at] + got(CARRY, d, p) + got(NEAR, 1 - d, p)).astype(BF16)
            share(p, d, d)
        for d in (RIGHT, LEFT):
            share(p, d, 1 - d)

        @pl.when(core == p)
        def _():
            y_ref[:, place(core, t, 0, block)] = yb[p]

        @pl.when(core != p)
        def _():
            remote(yb.at[p], y_ref.at[:, place(core, t, 0, block)], own_send, own_recv, dev(t, other)).start()

    def landed(d, h, k):
        at = place(k, (left, right)[d], h, TN)
        with jax.named_scope(f"land{d}{h}{k}"):
            remote(y_ref.at[:, at], y_ref.at[:, at], ag_send.at[0, d, h], ag_recv.at[d, h, k], dev(to[d], g)).wait_recv()
        return at

    for k in (0, 1):
        for d in (RIGHT, LEFT):
            at = landed(d, d, k)
            move = remote(y_ref.at[:, at], y_ref.at[:, at], fw_send.at[d, k], fw_recv.at[d, k], dev(to[d], g))
            move.start()
            sends.append(move)
    for k in (0, 1):
        for d in (RIGHT, LEFT):
            landed(d, 1 - d, k)
    at = place(1 - core, t, 0, block)
    sib = remote(yb.at[0], y_ref.at[:, at], own_send, own_recv, dev(t, other))
    sib.wait_recv()
    for k in (0, 1):
        for d in (RIGHT, LEFT):
            at = place(k, far, d, TN)
            with jax.named_scope(f"fw{d}{k}"):
                remote(y_ref.at[:, at], y_ref.at[:, at], fw_send.at[d, k], fw_recv.at[d, k], dev(to[d], g)).wait_recv()
    sib.wait_send()
    for move in x_moves + h_moves + sends:
        move.wait_send()


def solution(mesh):
    n = mesh.shape["tp"]

    def step(x, w_gate, w_up, w_down):
        rows, depth = x.shape
        hidden, out = w_down.shape
        half, cols = hidden // 2, out // 2
        steps = half // TK
        DMA = pltpu.SemaphoreType.DMA
        any_spec = pl.BlockSpec(memory_space=pl.ANY)
        return pl.pallas_call(
            functools.partial(kernel, n),
            out_shape=pltpu.VMEM((rows, out), BF16),
            in_specs=[any_spec] * 4,
            out_specs=pl.BlockSpec(memory_space=pltpu.VMEM),
            scratch_shapes=[
                pltpu.VMEM((2 * rows, depth), BF16),
                pltpu.VMEM((steps, depth, 2 * TK), BF16),
                pltpu.VMEM((n, hidden, cols // n), BF16),
                pltpu.VMEM((2, 2 * rows, 2 * TK), F32),
                pltpu.VMEM((2 * rows, hidden), BF16),
                pltpu.VMEM((2 * rows, cols // n), F32),
                pltpu.VMEM((2, 2 * rows, TN), F32),
                pltpu.VMEM((12, rows, TN), BF16),
                pltpu.VMEM((12, rows, TN), BF16),
                pltpu.VMEM((2, rows, 2 * TN), BF16),
                DMA((XP,)), DMA((XP,)), DMA((XP,)), DMA((steps, 2)), DMA((n, 2)), DMA((steps,)), DMA((steps,)),
                DMA((12,)), DMA((12,)), DMA((2, 2, 2)), DMA((2, 2, 2)), DMA((2, 2)), DMA((2, 2)), DMA, DMA,
            ],
            compiler_params=pltpu.CompilerParams(
                collective_id=0, has_side_effects=True, vmem_limit_bytes=56 * 1024 * 1024
            ),
        )(x, w_gate, w_up, w_down)

    return jax.shard_map(
        step,
        mesh=mesh,
        in_specs=(P("dp", None), P(None, "tp"), P(None, "tp"), P("tp", None)),
        out_specs=P("dp", None),
        check_vma=False,
    )
```

time: 48.6 us -> 35.5 us (0.73)
  Pallas kernels: 46.2 us -> 34.5 us
  local copies, waits for them, and re-layouts: 2.29 us -> 0.97 us
    pallas_call x1, Pallas kernels: 46.2 us -> 34.5 us  [step(): pl.pallas_call(functools.partial(kernel, n), out_shape=pltpu.VMEM((rows,...]
    unnamed x1, local copies, waits for them, and re-layouts: 2.29 us -> 0.97 us
where the time goes in v2:
time: 35.5 us
  Pallas kernels  34.5 us (97%)
  local copies, waits for them, and re-layouts  0.97 us (3%)
    pallas_call x1, Pallas kernels, step(): pl.pallas_call(functools.partial(kernel, n), out_shape=pltpu.VMEM((rows,...  34.5 us
    unnamed x1, local copies, waits for them, and re-layouts  0.97 us

profile of v2, /device:TPU:113, one launch (start us, length us, event | category | flops | bytes accessed | tf_op | source)
XLA Modules:
  0.0 35.5 jit_solution(7021338331629765829)
XLA Ops:
  0.0 34.5 %shard_map.46 = bf16[128,4096]{1,0:T(8,128)(2,1)S(1)} custom-call(bf16[128,4096]{1,0:T(8,128)(2,1)} %x_hbm.1, bf16[4096,2560]{1,0:T(8,128)(2,1)} %wg_hbm.1, bf16[4096,2560]{1,0:T(8,128)(2,1)} %wu_hbm.1, bf16[2560,4096]{1,0:T(8,128)(2,1)} %wd_hbm.1), custom_call_target="tpu_custom_call" | custom-call | tf_op jit(solution)/shard_map/pallas_call | solution.py:246
  34.5 1.0 %copy.6 = bf16[128,4096]{1,0:T(8,128)(2,1)} copy(bf16[128,4096]{1,0:T(8,128)(2,1)S(1)} %shard_map.46) | data formatting | bytes 2097152

commit v3 on v0

v3 whole, which is shorter than its diff:
```python
import functools

import jax
import jax.numpy as jnp
from jax import lax
from jax.experimental import pallas as pl
from jax.experimental.pallas import tpu as pltpu
from jax.sharding import PartitionSpec as P

MESH = pl.DeviceIdType.MESH
BF16 = jnp.bfloat16
F32 = jnp.float32
T = 256
Q = 4
FAR, NEAR, CARRY = 0, 1, 2
RIGHT, LEFT = 0, 1
OWN, HIS = 0, 1


def kernel(
    n, x_hbm, wg_hbm, wu_hbm, wd_hbm, y_ref,
    xv, wgu, wd, gacc, hid, far_sum, ysum, carry, stage, far_in, near_in, yb,
    x_sem, w_sem, d_sem, sent, x_recv, h_recv, far_recv, near_recv, pass_recv, end_recv, met,
):
    t = lax.axis_index("tp")
    g = lax.axis_index("dp")
    core = lax.rem(g, 2)
    other = g + 1 - 2 * core
    right, left = lax.rem(t + 1, n), lax.rem(t + n - 1, n)
    far = lax.rem(t + 2, n)
    rows, depth = x_hbm.shape
    half = wg_hbm.shape[1] // 2
    steps = half // T
    cols = wd_hbm.shape[1] // 2
    block = cols // n
    to = (right, left)

    def dev(tp, dp):
        return {"tp": tp, "dp": dp}

    def remote(src, dst, send, rcv, device):
        return pltpu.make_async_remote_copy(
            src_ref=src, dst_ref=dst, send_sem=send, recv_sem=rcv,
            device_id=device, device_id_type=MESH,
        )

    def start(copies):
        for copy in copies:
            copy.start(priority=1)

    def wait(copies, name):
        with jax.named_scope(name):
            for copy in copies:
                copy.wait()

    deep = [pl.ds(k * (depth // Q), depth // Q) for k in range(Q)]
    x_loads = [pltpu.make_async_copy(x_hbm.at[:, at], xv.at[OWN, :, at], x_sem.at[k]) for k, at in enumerate(deep)]
    for copy in x_loads:
        copy.start()
    upper, lower, full = pl.ds(0, depth // 2), pl.ds(depth // 2, depth // 2), pl.ds(0, depth)
    parts = [(j, at) for j in range(steps) for at in ((upper, lower) if j == 1 else (full,))]
    for i, (j, at) in enumerate(parts):
        start([pltpu.make_async_copy(
            w.at[at, pl.ds(pl.multiple_of(core * half + j * T, T), T)], wgu.at[j, at, pl.ds(q * T, T)], w_sem.at[i])
            for q, w in enumerate((wg_hbm, wu_hbm))])

    def load(i):
        j, at = parts[i]
        wait([pltpu.make_async_copy(wg_hbm.at[at, pl.ds(0, 2 * T)], wgu.at[j, at, :], w_sem.at[i])], f"w{i}")

    def take(sem, width):
        at = pl.ds(0, width)
        pltpu.make_async_copy(x_hbm.at[:, at], xv.at[OWN, :, at], sem).wait()

    d_loads = []
    for s, owner in enumerate((far, right, left, t)):
        at = pl.ds(pl.multiple_of(core * cols + owner * block, block), block)
        d_loads.append([
            pltpu.make_async_copy(
                wd_hbm.at[pl.ds(pl.multiple_of(c * half, half), half), at],
                wd.at[s, pl.ds(i * half, half), :], d_sem.at[s])
            for i, c in enumerate((core, 1 - core))])

    def load_down(s):
        wait([pltpu.make_async_copy(wd_hbm.at[:, pl.ds(0, block)], wd.at[s], d_sem.at[s])], f"d{s}")

    barrier = pltpu.get_barrier_semaphore()

    def signal(sem, device):
        pl.semaphore_signal(sem, inc=1, device_id=device, device_id_type=MESH)

    @pl.when(core == 0)
    def _():
        signal(barrier, dev(t, other))

    @pl.when(core == 1)
    def _():
        pl.semaphore_wait(barrier, 1)
        signal(met, dev(t, other))


    @pl.when(core == 0)
    def _():
        pl.semaphore_wait(met, 1)
        for a in to:
            signal(barrier, dev(a, g))

    for k, at in enumerate(deep):
        wait([x_loads[k]], "xl")
        remote(xv.at[OWN, :, at], xv.at[HIS, :, at], sent.at[0], x_recv, dev(t, other)).start()

    def dot(a, b):
        return jnp.dot(a, b, preferred_element_type=F32)

    def gate_up(j, rs, at=slice(None)):
        return dot(xv[rs, :, at], wgu[j, at, :])


    last = steps - 1

    def activate(j, rs, a):
        hid[rs, :, j * T : (j + 1) * T] = (jax.nn.gelu(a[:, :T]) * a[:, T:]).astype(BF16)

    def give(j, rs):
        remote(
            hid.at[rs, :, pl.ds(j * T, T)], hid.at[1 - rs, :, pl.ds(half + j * T, T)],
            sent.at[1], h_recv.at[1 - rs, j // last], dev(t, other)).start()

    both = (OWN, HIS)
    load(0)
    gacc[0] = gate_up(0, OWN)
    load(1)
    gacc[1] = gate_up(1, OWN, slice(0, depth // 2))
    load(2)
    with jax.named_scope("x"):
        take(x_recv, depth)
    activate(0, OWN, gacc[0])
    activate(0, HIS, gate_up(0, HIS))
    activate(1, OWN, gacc[1] + gate_up(1, OWN, slice(depth // 2, depth)))
    activate(1, HIS, gate_up(1, HIS))
    for j in (0, 1):
        for rs in both:
            give(j, rs)
    for j in range(2, last):
        load(j + 1)
        start(d_loads[j - 2])
        a = dot(xv[...].reshape(2 * rows, depth), wgu[j])
        for rs in both:
            activate(j, rs, a[rs * rows : (rs + 1) * rows])
        for rs in both:
            give(j, rs)
        if j == 2:

            @pl.when(core == 0)
            def _():
                pl.semaphore_wait(barrier, 2)
                signal(met, dev(t, other))

    load(last + 1)
    for s in range(last - 2, n):
        start(d_loads[s])
    for rs in (HIS, OWN):
        activate(last, rs, gate_up(last, rs))
        give(last, rs)

    @pl.when(core == 1)
    def _():
        pl.semaphore_wait(met, 1)

    def hop(kind, d, rs):
        dst, sem = {
            FAR: (far_in.at[d * 2 + rs], far_recv.at[d * 2 + rs]),
            CARRY: (near_in.at[d * 2 + rs, 0], near_recv.at[d * 2 + rs]),
            NEAR: (near_in.at[(1 - d) * 2 + rs, 1], near_recv.at[(1 - d) * 2 + rs]),
        }[kind]
        return remote(stage.at[(kind * 2 + d) * 2 + rs], dst, sent.at[2], sem, dev(to[d], g))

    def put(kind, d, rs, v):
        stage[(kind * 2 + d) * 2 + rs] = v.astype(BF16)

    def send(kind, d, rs):
        hop(kind, d, rs).start()

    load_down(0)
    most = 2 * half - T
    for rs in both:
        with jax.named_scope(f"h{rs}"):
            take(h_recv.at[rs, 0], last * T)
        far_sum[rs] = dot(hid[rs, :, :most], wd[0, :most, :])
        with jax.named_scope(f"hl{rs}"):
            take(h_recv.at[rs, 1], T)
        v = far_sum[rs] + dot(hid[rs, :, most:], wd[0, most:, :])
        for d in (RIGHT, LEFT):
            put(FAR, d, rs, v[:, d * T : (d + 1) * T])
        for d in (RIGHT, LEFT):
            send(FAR, d, rs)

    def down(s):
        return dot(hid[...].reshape(2 * rows, 2 * half), wd[s])

    for d in (RIGHT, LEFT):
        load_down(1 + d)
        v = down(1 + d)
        for rs in both:
            put(NEAR, d, rs, v[rs * rows : (rs + 1) * rows, (1 - d) * T : (2 - d) * T])
            carry[d, rs] = v[rs * rows : (rs + 1) * rows, d * T : (d + 1) * T]
        send(NEAR, d, OWN)
    load_down(3)
    v = down(3)
    for rs in both:
        ysum[rs] = v[rs * rows : (rs + 1) * rows]

    for rs in both:
        for d in (RIGHT, LEFT):
            with jax.named_scope(f"far{d}{rs}"):
                take(far_recv.at[d * 2 + rs], T)
            put(CARRY, d, rs, carry[d, rs] + far_in[d * 2 + rs].astype(F32))
            send(CARRY, d, rs)
        if rs == OWN:
            for d in (RIGHT, LEFT):
                send(NEAR, d, HIS)

    def place(k, owner, h, width):
        return pl.ds(pl.multiple_of(k * cols + owner * block + h * T, T), width)

    def share(rs, d, h):
        at = place(core, t, h, T)
        remote(yb.at[rs, :, pl.ds(h * T, T)], y_ref.at[:, at], sent.at[3],
               pass_recv.at[rs, d] if d == h else end_recv, dev(to[d], (g, other)[rs])).start()

    mine = place(core, t, 0, block)
    for rs in both:
        for d in (RIGHT, LEFT):
            i = d * 2 + rs
            with jax.named_scope(f"near{d}{rs}"):
                take(near_recv.at[i], 2 * T)
            yb[rs, :, d * T : (d + 1) * T] = (
                ysum[rs, :, d * T : (d + 1) * T] + near_in[i, 0].astype(F32) + near_in[i, 1].astype(F32)).astype(BF16)
            share(rs, d, d)
        for d in (RIGHT, LEFT):
            share(rs, d, 1 - d)
        if rs == OWN:
            y_ref[:, mine] = yb[OWN]
        else:
            remote(yb.at[HIS], y_ref.at[:, mine], sent.at[3], end_recv, dev(t, other)).start()

    for rs in both:
        for d in (RIGHT, LEFT):
            with jax.named_scope(f"pass{d}{rs}"):
                take(pass_recv.at[rs, d], T)
            at = place((core, 1 - core)[rs], (left, right)[d], d, T)
            remote(y_ref.at[:, at], y_ref.at[:, at], sent.at[4], end_recv, dev(to[d], g)).start()
    with jax.named_scope("end"):
        take(end_recv, 8 * T + block)
    with jax.named_scope("sends"):
        for i, width in enumerate((depth, 2 * half, 12 * T, 8 * T + block, 4 * T)):
            take(sent.at[i], width)


def solution(mesh):
    n = mesh.shape["tp"]

    def step(x, w_gate, w_up, w_down):
        rows, depth = x.shape
        hidden, out = w_down.shape
        steps, block = hidden // 2 // T, out // 2 // n
        DMA = pltpu.SemaphoreType.DMA
        hbm = pl.BlockSpec(memory_space=pl.ANY)
        return pl.pallas_call(
            functools.partial(kernel, n),
            out_shape=pltpu.VMEM((rows, out), BF16),
            in_specs=[hbm] * 4,
            out_specs=pl.BlockSpec(memory_space=pltpu.VMEM),
            scratch_shapes=[
                pltpu.VMEM((2, rows, depth), BF16),
                pltpu.VMEM((steps, depth, 2 * T), BF16),
                pltpu.VMEM((n, hidden, block), BF16),
                pltpu.VMEM((2, rows, 2 * T), F32),
                pltpu.VMEM((2, rows, hidden), BF16),
                pltpu.VMEM((2, rows, block), F32),
                pltpu.VMEM((2, rows, block), F32),
                pltpu.VMEM((2, 2, rows, T), F32),
                pltpu.VMEM((12, rows, T), BF16),
                pltpu.VMEM((4, rows, T), BF16),
                pltpu.VMEM((4, 2, rows, T), BF16),
                pltpu.VMEM((2, rows, block), BF16),
                DMA((Q,)), DMA((steps + 1,)), DMA((n,)), DMA((5,)),
                DMA, DMA((2, 2)), DMA((4,)), DMA((4,)), DMA((2, 2)), DMA, pltpu.SemaphoreType.REGULAR,
            ],
            compiler_params=pltpu.CompilerParams(
                collective_id=0, has_side_effects=True, vmem_limit_bytes=56 * 1024 * 1024
            ),
        )(x, w_gate, w_up, w_down)

    return jax.shard_map(
        step,
        mesh=mesh,
        in_specs=(P("dp", None), P(None, "tp"), P(None, "tp"), P("tp", None)),
        out_specs=P("dp", None),
        check_vma=False,
    )
```

time: 84.1 us -> 33.3 us (0.40)
  the two profiles are of different devices: /device:TPU:112 before, /device:TPU:113 now
where the time goes in v3:
time: 33.3 us; the launch traced here: 33 us
  Pallas kernels  32 us (96%)
  local copies, waits for them, and re-layouts  0.97 us (3%)
    pallas_call x1, Pallas kernels, step(): pl.pallas_call(functools.partial(kernel, n), out_shape=pltpu.VMEM((rows,...  32 us
    unnamed x1, local copies, waits for them, and re-layouts  0.97 us

profile of v3, /device:TPU:113, one launch (start us, length us, event | category | flops | bytes accessed | tf_op | source)
XLA Modules:
  0.0 33.0 jit_solution(3148596898958646010)
XLA Ops:
  0.0 32.0 %shard_map.46 = bf16[128,4096]{1,0:T(8,128)(2,1)S(1)} custom-call(bf16[128,4096]{1,0:T(8,128)(2,1)} %x_hbm.1, bf16[4096,2560]{1,0:T(8,128)(2,1)} %wg_hbm.1, bf16[4096,2560]{1,0:T(8,128)(2,1)} %wu_hbm.1, bf16[2560,4096]{1,0:T(8,128)(2,1)} %wd_hbm.1), custom_call_target="tpu_custom_call" | custom-call | tf_op jit(solution)/shard_map/pallas_call | solution.py:269
  32.0 1.0 %copy.6 = bf16[128,4096]{1,0:T(8,128)(2,1)} copy(bf16[128,4096]{1,0:T(8,128)(2,1)S(1)} %shard_map.46) | data formatting | bytes 2097152

commit v4 on v3

v4 whole, which is shorter than its diff:
```python
import functools

import jax
import jax.numpy as jnp
from jax import lax
from jax.experimental import pallas as pl
from jax.experimental.pallas import tpu as pltpu
from jax.sharding import PartitionSpec as P

MESH = pl.DeviceIdType.MESH
BF16 = jnp.bfloat16
F32 = jnp.float32
T = 256
Q = 4
FAR, NEAR, CARRY = 0, 1, 2
RIGHT, LEFT = 0, 1


def kernel(n, *refs):
    DMA = pltpu.SemaphoreType.DMA
    steps = refs[1].shape[1] // 2 // T
    pl.run_scoped(functools.partial(body, n, *refs), DMA((Q,)), DMA((steps + 1,)), DMA((n,)), DMA((5,)))


def body(
    n, x_hbm, wg_hbm, wu_hbm, wd_hbm, y_ref,
    xv, wgu, wd, gacc, hid, far_sum, ysum, carry, stage, far_in, near_in, yb,
    x_recv, h_recv, far_recv, near_recv, pass_recv, end_recv, met,
    x_sem, w_sem, d_sem, sent,
):
    t = lax.axis_index("tp")
    g = lax.axis_index("dp")
    core = lax.rem(g, 2)
    groups = (g - core, g - core + 1)
    other = g + 1 - 2 * core
    right, left = lax.rem(t + 1, n), lax.rem(t + n - 1, n)
    far = lax.rem(t + 2, n)
    rows, depth = x_hbm.shape
    half = wg_hbm.shape[1] // 2
    steps = half // T
    cols = wd_hbm.shape[1] // 2
    block = cols // n
    to = (right, left)

    def dev(tp, dp):
        return {"tp": tp, "dp": dp}

    def remote(src, dst, send, rcv, device):
        return pltpu.make_async_remote_copy(
            src_ref=src, dst_ref=dst, send_sem=send, recv_sem=rcv,
            device_id=device, device_id_type=MESH,
        )

    def start(copies):
        for copy in copies:
            copy.start(priority=1)

    def wait(copies, name):
        with jax.named_scope(name):
            for copy in copies:
                copy.wait()

    deep = [pl.ds(k * (depth // Q), depth // Q) for k in range(Q)]
    x_loads = [pltpu.make_async_copy(x_hbm.at[:, at], xv.at[core, :, at], x_sem.at[k]) for k, at in enumerate(deep)]
    for copy in x_loads:
        copy.start()
    upper, lower, full = pl.ds(0, depth // 2), pl.ds(depth // 2, depth // 2), pl.ds(0, depth)
    parts = [(j, at) for j in range(steps) for at in ((upper, lower) if j == 1 else (full,))]
    for i, (j, at) in enumerate(parts):
        start([pltpu.make_async_copy(
            w.at[at, pl.ds(pl.multiple_of(core * half + j * T, T), T)], wgu.at[j, at, pl.ds(q * T, T)], w_sem.at[i])
            for q, w in enumerate((wg_hbm, wu_hbm))])

    def load(i):
        j, at = parts[i]
        wait([pltpu.make_async_copy(wg_hbm.at[at, pl.ds(0, 2 * T)], wgu.at[j, at, :], w_sem.at[i])], f"w{i}")

    def take(sem, width):
        at = pl.ds(0, width)
        pltpu.make_async_copy(x_hbm.at[:, at], xv.at[0, :, at], sem).wait()

    d_loads = []
    for s, owner in enumerate((far, right, left, t)):
        at = pl.ds(pl.multiple_of(core * cols + owner * block, block), block)
        d_loads.append([
            pltpu.make_async_copy(
                wd_hbm.at[pl.ds(pl.multiple_of(c * half, half), half), at],
                wd.at[s, pl.ds(i * half, half), :], d_sem.at[s])
            for i, c in enumerate((core, 1 - core))])

    def load_down(s):
        wait([pltpu.make_async_copy(wd_hbm.at[:, pl.ds(0, block)], wd.at[s], d_sem.at[s])], f"d{s}")

    barrier = pltpu.get_barrier_semaphore()

    def signal(sem, device):
        pl.semaphore_signal(sem, inc=1, device_id=device, device_id_type=MESH)

    @pl.when(core == 0)
    def _():
        signal(barrier, dev(t, other))

    @pl.when(core == 1)
    def _():
        pl.semaphore_wait(barrier, 1)
        signal(met, dev(t, other))


    @pl.when(core == 0)
    def _():
        pl.semaphore_wait(met, 1)
        for a in to:
            signal(barrier, dev(a, g))

    for k, at in enumerate(deep):
        wait([x_loads[k]], "xl")
        remote(xv.at[core, :, at], xv.at[core, :, at], sent.at[0], x_recv, dev(t, other)).start()

    def dot(a, b):
        return jnp.dot(a, b, preferred_element_type=F32)

    def gate_up(j, p, at=slice(None)):
        return dot(xv[p, :, at], wgu[j, at, :])

    last = steps - 1

    def activate(j, p, a):
        hid[p, :, j * T : (j + 1) * T] = (jax.nn.gelu(a[:, :T]) * a[:, T:]).astype(BF16)

    def give(j, p):
        remote(
            hid.at[p, :, pl.ds(j * T, T)], hid.at[p, :, pl.ds(half + j * T, T)],
            sent.at[1], h_recv.at[p, j // last], dev(t, other)).start()

    both = (0, 1)
    load(0)
    gacc[0] = gate_up(0, core)
    load(1)
    gacc[1] = gate_up(1, core, slice(0, depth // 2))
    load(2)
    with jax.named_scope("x"):
        take(x_recv, depth)
    activate(0, core, gacc[0])
    activate(0, 1 - core, gate_up(0, 1 - core))
    activate(1, core, gacc[1] + gate_up(1, core, slice(depth // 2, depth)))
    activate(1, 1 - core, gate_up(1, 1 - core))
    for j in (0, 1):
        for p in both:
            give(j, p)
    for j in range(2, last - 1):
        load(j + 1)
        start(d_loads[j - 2])
        a = dot(xv[...].reshape(2 * rows, depth), wgu[j])
        for p in both:
            activate(j, p, a[p * rows : (p + 1) * rows])
        for p in both:
            give(j, p)

    @pl.when(core == 0)
    def _():
        pl.semaphore_wait(barrier, 2)
        signal(met, dev(t, other))

    load(last)
    for s in range(last - 3, n):
        start(d_loads[s])
    activate(last - 1, 0, gate_up(last - 1, 0))
    give(last - 1, 0)
    load(last + 1)
    activate(last, 0, gate_up(last, 0))
    give(last, 0)
    activate(last - 1, 1, gate_up(last - 1, 1))
    give(last - 1, 1)

    @pl.when(core == 1)
    def _():
        pl.semaphore_wait(met, 1)

    def hop(kind, d, rs):
        dst, sem = {
            FAR: (far_in.at[d * 2 + rs], far_recv.at[d * 2 + rs]),
            CARRY: (near_in.at[d * 2 + rs, 0], near_recv.at[d * 2 + rs]),
            NEAR: (near_in.at[(1 - d) * 2 + rs, 1], near_recv.at[(1 - d) * 2 + rs]),
        }[kind]
        return remote(stage.at[(kind * 2 + d) * 2 + rs], dst, sent.at[2], sem, dev(to[d], g))

    def put(kind, d, rs, v):
        stage[(kind * 2 + d) * 2 + rs] = v.astype(BF16)

    def send(kind, d, rs):
        hop(kind, d, rs).start()

    most = 2 * half - T

    def far_block(p):
        with jax.named_scope(f"h{p}"):
            take(h_recv.at[p, 0], last * T)
        far_sum[p] = dot(hid[p, :, :most], wd[0, :most, :])
        with jax.named_scope(f"hl{p}"):
            take(h_recv.at[p, 1], T)
        v = far_sum[p] + dot(hid[p, :, most:], wd[0, most:, :])
        for d in (RIGHT, LEFT):
            put(FAR, d, p, v[:, d * T : (d + 1) * T])
        for d in (RIGHT, LEFT):
            send(FAR, d, p)

    def down(s, p, d):
        return dot(hid[p], wd[s, :, d * T : (d + 1) * T])

    load_down(0)
    far_block(0)
    activate(last, 1, gate_up(last, 1))
    give(last, 1)
    load_down(1)
    load_down(2)
    for d in (RIGHT, LEFT):
        put(NEAR, d, 0, down(1 + d, 0, 1 - d))
    for d in (RIGHT, LEFT):
        send(NEAR, d, 0)
    far_block(1)
    for d in (RIGHT, LEFT):
        carry[d, 0] = down(1 + d, 0, d)
        carry[d, 1] = down(1 + d, 1, d)
        put(NEAR, d, 1, down(1 + d, 1, 1 - d))
    for p in both:
        for d in (RIGHT, LEFT):
            with jax.named_scope(f"far{d}{p}"):
                take(far_recv.at[d * 2 + p], T)
            put(CARRY, d, p, carry[d, p] + far_in[d * 2 + p].astype(F32))
            send(CARRY, d, p)
        if p == 0:
            for d in (RIGHT, LEFT):
                send(NEAR, d, 1)
            load_down(3)
            v = dot(hid[...].reshape(2 * rows, 2 * half), wd[3])
            for r in both:
                ysum[r] = v[r * rows : (r + 1) * rows]

    def place(k, owner, h, width):
        return pl.ds(pl.multiple_of(k * cols + owner * block + h * T, T), width)

    def share(p, d, h):
        at = place(core, t, h, T)
        remote(yb.at[p, :, pl.ds(h * T, T)], y_ref.at[:, at], sent.at[3],
               pass_recv.at[core, d] if d == h else end_recv, dev(to[d], groups[p])).start()

    mine = place(core, t, 0, block)
    for p in both:
        for d in (RIGHT, LEFT):
            i = d * 2 + p
            with jax.named_scope(f"near{d}{p}"):
                take(near_recv.at[i], 2 * T)
            yb[p, :, d * T : (d + 1) * T] = (
                ysum[p, :, d * T : (d + 1) * T] + near_in[i, 0].astype(F32) + near_in[i, 1].astype(F32)).astype(BF16)
            share(p, d, d)
        for d in (RIGHT, LEFT):
            share(p, d, 1 - d)
    y_ref[:, mine] = yb[core]
    remote(yb.at[1 - core], y_ref.at[:, mine], sent.at[3], end_recv, dev(t, other)).start()

    for p in both:
        for d in (RIGHT, LEFT):
            with jax.named_scope(f"pass{d}{p}"):
                take(pass_recv.at[p, d], T)
            at = place(p, (left, right)[d], d, T)
            remote(y_ref.at[:, at], y_ref.at[:, at], sent.at[4], end_recv, dev(to[d], g)).start()
    with jax.named_scope("end"):
        take(end_recv, 8 * T + block)
    with jax.named_scope("sends"):
        for i, width in enumerate((depth, 2 * half, 12 * T, 8 * T + block, 4 * T)):
            take(sent.at[i], width)


def solution(mesh):
    n = mesh.shape["tp"]

    def step(x, w_gate, w_up, w_down):
        rows, depth = x.shape
        hidden, out = w_down.shape
        steps, block = hidden // 2 // T, out // 2 // n
        DMA = pltpu.SemaphoreType.DMA
        hbm = pl.BlockSpec(memory_space=pl.ANY)
        return pl.pallas_call(
            functools.partial(kernel, n),
            out_shape=pltpu.VMEM((rows, out), BF16),
            in_specs=[hbm] * 4,
            out_specs=pl.BlockSpec(memory_space=pltpu.VMEM),
            scratch_shapes=[
                pltpu.VMEM((2, rows, depth), BF16),
                pltpu.VMEM((steps, depth, 2 * T), BF16),
                pltpu.VMEM((n, hidden, block), BF16),
                pltpu.VMEM((2, rows, 2 * T), F32),
                pltpu.VMEM((2, rows, hidden), BF16),
                pltpu.VMEM((2, rows, block), F32),
                pltpu.VMEM((2, rows, block), F32),
                pltpu.VMEM((2, 2, rows, T), F32),
                pltpu.VMEM((12, rows, T), BF16),
                pltpu.VMEM((4, rows, T), BF16),
                pltpu.VMEM((4, 2, rows, T), BF16),
                pltpu.VMEM((2, rows, block), BF16),
                DMA, DMA((2, 2)), DMA((4,)), DMA((4,)), DMA((2, 2)), DMA, pltpu.SemaphoreType.REGULAR,
            ],
            compiler_params=pltpu.CompilerParams(
                collective_id=0, has_side_effects=True, vmem_limit_bytes=56 * 1024 * 1024
            ),
        )(x, w_gate, w_up, w_down)

    return jax.shard_map(
        step,
        mesh=mesh,
        in_specs=(P("dp", None), P(None, "tp"), P(None, "tp"), P("tp", None)),
        out_specs=P("dp", None),
        check_vma=False,
    )
```

time: 33.3 us -> 32.6 us (0.979)
  Pallas kernels: 32 us -> 31.5 us
    pallas_call x1, Pallas kernels: 32 us -> 31.5 us  [step(): pl.pallas_call(functools.partial(kernel, n), out_shape=pltpu.VMEM((rows,...]
where the time goes in v4:
time: 32.6 us; the launch traced here: 32.5 us
  Pallas kernels  31.5 us (97%)
  local copies, waits for them, and re-layouts  0.97 us (3%)
    pallas_call x1, Pallas kernels, step(): pl.pallas_call(functools.partial(kernel, n), out_shape=pltpu.VMEM((rows,...  31.5 us
    unnamed x1, local copies, waits for them, and re-layouts  0.97 us

profile of v4, /device:TPU:113, one launch (start us, length us, event | category | flops | bytes accessed | tf_op | source)
XLA Modules:
  0.0 32.5 jit_solution(15098229012699228130)
XLA Ops:
  0.0 31.5 %shard_map.46 = bf16[128,4096]{1,0:T(8,128)(2,1)S(1)} custom-call(bf16[128,4096]{1,0:T(8,128)(2,1)} %refs_0_.1, bf16[4096,2560]{1,0:T(8,128)(2,1)} %refs_1_.1, bf16[4096,2560]{1,0:T(8,128)(2,1)} %refs_2_.1, bf16[2560,4096]{1,0:T(8,128)(2,1)} %refs_3_.1), custom_call_target="tpu_custom_call" | custom-call | tf_op jit(solution)/shard_map/pallas_call | solution.py:283
  31.5 1.0 %copy.6 = bf16[128,4096]{1,0:T(8,128)(2,1)} copy(bf16[128,4096]{1,0:T(8,128)(2,1)S(1)} %shard_map.46) | data formatting | bytes 2097152

commit v5 on v4

--- a/solution.py
+++ b/solution.py
@@ -19,14 +19,17 @@
 def kernel(n, *refs):
     DMA = pltpu.SemaphoreType.DMA
     steps = refs[1].shape[1] // 2 // T
-    pl.run_scoped(functools.partial(body, n, *refs), DMA((Q,)), DMA((steps + 1,)), DMA((n,)), DMA((5,)))
+    pl.run_scoped(
+        functools.partial(body, n, *refs),
+        DMA((Q,)), DMA((steps + 1,)), DMA((n,)), DMA((5,)),
+        DMA, DMA((2, 2)), DMA((4,)), DMA((4,)), DMA((2, 2)), DMA,
+    )
 
 
 def body(
     n, x_hbm, wg_hbm, wu_hbm, wd_hbm, y_ref,
     xv, wgu, wd, gacc, hid, far_sum, ysum, carry, stage, far_in, near_in, yb,
-    x_recv, h_recv, far_recv, near_recv, pass_recv, end_recv, met,
-    x_sem, w_sem, d_sem, sent,
+    met, x_sem, w_sem, d_sem, sent, x_recv, h_recv, far_recv, near_recv, pass_recv, end_recv,
 ):
     t = lax.axis_index("tp")
     g = lax.axis_index("dp")
@@ -278,7 +281,6 @@
         rows, depth = x.shape
         hidden, out = w_down.shape
         steps, block = hidden // 2 // T, out // 2 // n
-        DMA = pltpu.SemaphoreType.DMA
         hbm = pl.BlockSpec(memory_space=pl.ANY)
         return pl.pallas_call(
             functools.partial(kernel, n),
@@ -298,7 +300,7 @@
                 pltpu.VMEM((4, rows, T), BF16),
                 pltpu.VMEM((4, 2, rows, T), BF16),
                 pltpu.VMEM((2, rows, block), BF16),
-                DMA, DMA((2, 2)), DMA((4,)), DMA((4,)), DMA((2, 2)), DMA, pltpu.SemaphoreType.REGULAR,
+                pltpu.SemaphoreType.REGULAR,
             ],
             compiler_params=pltpu.CompilerParams(
                 collective_id=0, has_side_effects=True, vmem_limit_bytes=56 * 1024 * 1024

time: 32.6 us -> 32.4 us (level)
  no operation moved by 1% of the time
where the time goes in v5:
time: 32.4 us; the launch traced here: 32.3 us
  Pallas kernels  31.4 us (97%)
  local copies, waits for them, and re-layouts  0.97 us (3%)
    pallas_call x1, Pallas kernels, step(): pl.pallas_call(functools.partial(kernel, n), out_shape=pltpu.VMEM((rows,...  31.4 us
    unnamed x1, local copies, waits for them, and re-layouts  0.97 us

profile of v5, /device:TPU:113, one launch (start us, length us, event | category | flops | bytes accessed | tf_op | source)
XLA Modules:
  0.0 32.3 jit_solution(10320762073561776529)
XLA Ops:
  0.0 31.4 %shard_map.46 = bf16[128,4096]{1,0:T(8,128)(2,1)S(1)} custom-call(bf16[128,4096]{1,0:T(8,128)(2,1)} %refs_0_.1, bf16[4096,2560]{1,0:T(8,128)(2,1)} %refs_1_.1, bf16[4096,2560]{1,0:T(8,128)(2,1)} %refs_2_.1, bf16[2560,4096]{1,0:T(8,128)(2,1)} %refs_3_.1), custom_call_target="tpu_custom_call" | custom-call | tf_op jit(solution)/shard_map/pallas_call | solution.py:285
  31.4 1.0 %copy.6 = bf16[128,4096]{1,0:T(8,128)(2,1)} copy(bf16[128,4096]{1,0:T(8,128)(2,1)S(1)} %shard_map.46) | data formatting | bytes 2097152

commit v6 on v5

--- a/solution.py
+++ b/solution.py
@@ -133,7 +133,7 @@
     def give(j, p):
         remote(
             hid.at[p, :, pl.ds(j * T, T)], hid.at[p, :, pl.ds(half + j * T, T)],
-            sent.at[1], h_recv.at[p, j // last], dev(t, other)).start()
+            sent.at[1], h_recv.at[p, int(j >= last - p)], dev(t, other)).start()
 
     both = (0, 1)
     load(0)
@@ -172,8 +172,7 @@
     load(last + 1)
     activate(last, 0, gate_up(last, 0))
     give(last, 0)
-    activate(last - 1, 1, gate_up(last - 1, 1))
-    give(last - 1, 1)
+    gacc[0] = gate_up(last - 1, 1, slice(0, depth // 2))
 
     @pl.when(core == 1)
     def _():
@@ -193,14 +192,14 @@
     def send(kind, d, rs):
         hop(kind, d, rs).start()
 
-    most = 2 * half - T
 
     def far_block(p):
         with jax.named_scope(f"h{p}"):
-            take(h_recv.at[p, 0], last * T)
+            take(h_recv.at[p, 0], (last - p) * T)
+        most = 2 * half - (1 + p) * T
         far_sum[p] = dot(hid[p, :, :most], wd[0, :most, :])
         with jax.named_scope(f"hl{p}"):
-            take(h_recv.at[p, 1], T)
+            take(h_recv.at[p, 1], (1 + p) * T)
         v = far_sum[p] + dot(hid[p, :, most:], wd[0, most:, :])
         for d in (RIGHT, LEFT):
             put(FAR, d, p, v[:, d * T : (d + 1) * T])
@@ -212,17 +211,20 @@
 
     load_down(0)
     far_block(0)
-    activate(last, 1, gate_up(last, 1))
-    give(last, 1)
     load_down(1)
     load_down(2)
+    activate(last - 1, 1, gacc[0] + gate_up(last - 1, 1, slice(depth // 2, depth)))
+    activate(last, 1, gate_up(last, 1))
     for d in (RIGHT, LEFT):
         put(NEAR, d, 0, down(1 + d, 0, 1 - d))
+    give(last - 1, 1)
+    give(last, 1)
     for d in (RIGHT, LEFT):
         send(NEAR, d, 0)
+    for d in (RIGHT, LEFT):
+        carry[d, 0] = down(1 + d, 0, d)
     far_block(1)
     for d in (RIGHT, LEFT):
-        carry[d, 0] = down(1 + d, 0, d)
         carry[d, 1] = down(1 + d, 1, d)
         put(NEAR, d, 1, down(1 + d, 1, 1 - d))
     for p in both:

time: 32.4 us -> 32.9 us (1.015)
  Pallas kernels: 31.4 us -> 31.8 us
    pallas_call x1, Pallas kernels: 31.4 us -> 31.8 us  [step(): pl.pallas_call(functools.partial(kernel, n), out_shape=pltpu.VMEM((rows,...]
where the time goes in v6:
time: 32.9 us; the launch traced here: 32.8 us
  Pallas kernels  31.8 us (97%)
  local copies, waits for them, and re-layouts  0.97 us (3%)
    pallas_call x1, Pallas kernels, step(): pl.pallas_call(functools.partial(kernel, n), out_shape=pltpu.VMEM((rows,...  31.8 us
    unnamed x1, local copies, waits for them, and re-layouts  0.97 us

profile of v6, /device:TPU:113, one launch (start us, length us, event | category | flops | bytes accessed | tf_op | source)
XLA Modules:
  0.0 32.8 jit_solution(16504020724435052247)
XLA Ops:
  0.0 31.8 %shard_map.46 = bf16[128,4096]{1,0:T(8,128)(2,1)S(1)} custom-call(bf16[128,4096]{1,0:T(8,128)(2,1)} %refs_0_.1, bf16[4096,2560]{1,0:T(8,128)(2,1)} %refs_1_.1, bf16[4096,2560]{1,0:T(8,128)(2,1)} %refs_2_.1, bf16[2560,4096]{1,0:T(8,128)(2,1)} %refs_3_.1), custom_call_target="tpu_custom_call" | custom-call | tf_op jit(solution)/shard_map/pallas_call | solution.py:287
  31.8 1.0 %copy.6 = bf16[128,4096]{1,0:T(8,128)(2,1)} copy(bf16[128,4096]{1,0:T(8,128)(2,1)S(1)} %shard_map.46) | data formatting | bytes 2097152
